TPU v7x, 32 devices: a whole 2x2x4 slice. The times are simulated.
32 devices in a mesh: dp: 2 (over x), ep: 4 (over z), tp: 4 (over y, core).
Axes of the slice: x: 2, y: 2, z: 4, core: 2. Of those that a mesh axis runs over, the one named last changes fastest.
Arguments:
- tokens: bfloat16 [1536, 2560], P(('dp', 'ep', 'tp')), parts along dimension 0
- expert_ids: int32 [1536, 6], P(('dp', 'ep', 'tp')), parts along dimension 0
- gate_vals: float32 [1536, 6], P(('dp', 'ep', 'tp')), parts along dimension 0
- w_gate: bfloat16 [64, 2560, 1536], P('ep', None, 'tp')
- w_up: bfloat16 [64, 2560, 1536], P('ep', None, 'tp')
- w_down: bfloat16 [64, 1536, 2560], P('ep', 'tp')
Outputs:
- output: bfloat16 [1536, 2560], P(('dp', 'ep', 'tp')), parts along dimension 0
There are 2 independent parts. A program takes and returns all parts, laid end to end along the dimension named above; an argument that names none is the same for every part.
All inputs are finite; a program needn't handle non-finite values.
Results may differ from a plain program's by a relative error of at most 0.0101411.
Values are sent between devices in bfloat16 or wider.
A program may use at most 1 GiB of HBM per device.

v0:
```python
import jax
import jax.numpy as jnp
from jax import lax
from jax.sharding import PartitionSpec as P

CAP_FACTOR = 2


def slot_table(ids_loc, n_exp):
    tok_loc, n_top = ids_loc.shape
    flat_ids = ids_loc.reshape(tok_loc * n_top)
    one_hot = (flat_ids[:, None] == jnp.arange(n_exp, dtype=jnp.int32)[None, :]).astype(jnp.int32)
    preceding = jnp.cumsum(one_hot, axis=0) - one_hot
    return jnp.sum(preceding * one_hot, axis=1).reshape(tok_loc, n_top)


def dispatch_plan(ids_loc, n_exp, capacity):
    tok_loc, n_top = ids_loc.shape
    slot_ids = slot_table(ids_loc, n_exp)
    kept_mask = slot_ids < capacity
    flat_pos = jnp.where(kept_mask, ids_loc * capacity + slot_ids, n_exp * capacity)
    tok_index = jnp.broadcast_to(jnp.arange(tok_loc, dtype=jnp.int32)[:, None], (tok_loc, n_top))
    src_rows = jnp.zeros((n_exp * capacity,), jnp.int32).at[flat_pos.reshape(-1)].set(tok_index.reshape(-1), mode="drop")
    return src_rows, flat_pos, kept_mask


def combine_rows(y_slots, flat_pos, kept_mask, gate_loc):
    picked = jnp.take(y_slots, jnp.where(kept_mask, flat_pos, 0), axis=0)
    weights = jnp.where(kept_mask, gate_loc, 0.0)
    return jnp.sum(picked.astype(jnp.float32) * weights[:, :, None], axis=1)


def solution(mesh):
    expert_ranks = mesh.shape["ep"]
    row_spec = P(("dp", "ep", "tp"), None)

    def local_layer(x_loc, ids_loc, gate_loc, wg_loc, wu_loc, wd_loc):
        tok_loc, d_model = x_loc.shape
        n_top = ids_loc.shape[1]
        local_exp = wg_loc.shape[0]
        n_exp = local_exp * expert_ranks
        capacity = CAP_FACTOR * n_top * tok_loc // n_exp
        src_rows, flat_pos, kept_mask = dispatch_plan(ids_loc, n_exp, capacity)
        send_rows = jnp.take(x_loc, src_rows, axis=0).reshape(expert_ranks, local_exp, capacity, d_model)
        recv_rows = lax.all_to_all(send_rows, "ep", 0, 2, tiled=True)[0]
        group_rows = lax.all_gather(recv_rows, "tp", axis=1, tiled=True)
        gate_pre = jnp.einsum("erd,edf->erf", group_rows, wg_loc, preferred_element_type=jnp.float32)
        up_pre = jnp.einsum("erd,edf->erf", group_rows, wu_loc, preferred_element_type=jnp.float32)
        hidden = (jax.nn.silu(gate_pre) * up_pre).astype(jnp.bfloat16)
        part_sums = jnp.einsum("erf,efd->erd", hidden, wd_loc, preferred_element_type=jnp.float32).astype(jnp.bfloat16)
        pieces = lax.all_to_all(part_sums[None], "tp", 2, 0, tiled=True)
        y_rows = jnp.sum(pieces.astype(jnp.float32), axis=0).astype(jnp.bfloat16)
        returned = lax.all_to_all(y_rows[None], "ep", 2, 0, tiled=True)
        y_slots = returned.reshape(n_exp * capacity, d_model)
        return combine_rows(y_slots, flat_pos, kept_mask, gate_loc).astype(jnp.bfloat16)

    return jax.shard_map(local_layer, mesh=mesh, in_specs=(row_spec, row_spec, row_spec, P("ep", None, "tp"), P("ep", None, "tp"), P("ep", "tp", None)), out_specs=row_spec, check_vma=False)
```

profile of v0, /device:TPU:0, one launch (start us, length us, event | category | flops | bytes accessed | tf_op | source)
XLA Modules:
  0.0 486.5 jit_solution(11295924070383297001)
XLA Ops:
  6.5 0.7 broadcast_multiply_fusion
  7.3 0.8 copy.20
  8.4 0.9 reduce-window.6
  9.3 0.2 slice_reduce_fusion
  10.0 2.9 scatter_custom_fusion
  13.2 3.6 gather_fusion
  16.8 3.2 gather.11
  20.0 3.0 broadcast_select_fusion
  23.1 1.8 copy.25
  24.9 72.6 %all_to_all.42 = bf16[4,16,9,2560]{3,1,2,0:T(8,128)(2,1)} all-to-all(bf16[4,16,9,2560]{3,1,2,0:T(8,128)(2,1)S(1)} %copy.25), channel_id=1, replica_groups=mesh['dp'=2,'ep'=4,'tp'=4] {'ep'}, dimensions={0} | all-to-all | bytes 5898240 | tf_op jit(solution)/shard_map/all_to_all | solution.py:45
  97.5 77.6 %all-gather.2.cloned.1.call-done = bf16[16,144,2560]{2,0,1:T(8,128)(2,1)} async-done(((bf16[16,36,2560]{2,0,1:T(8,128)(2,1)}), bf16[16,144,2560]{2,0,1:T(8,128)(2,1)}) %all-gather.2.cloned.1.call-update) | async-done | bytes 11796496 | tf_op jit(solution)/shard_map/all_gather | solution.py:46
  175.1 21.1 %fusion = f32[16,144,384]{2,1,0:T(8,128)} fusion(bf16[16,2560,384]{2,1,0:T(8,128)(2,1)} %param.10, bf16[16,144,2560]{2,0,1:T(8,128)(2,1)} %all-gather.2.cloned.1.call-done), kind=kOutput, calls=%fused_computation.4 | convolution fusion | flops 4529848320 | bytes 46792704 | tf_op jit(solution)/shard_map/erd,edf->erf/dot_general | solution.py:48
  196.2 20.8 %multiply_convert_fusion.clone.4 = bf16[16,144,384]{2,1,0:T(8,128)(2,1)S(1)} fusion(f32[16,144,384]{2,1,0:T(8,128)} %fusion, bf16[16,2560,384]{2,1,0:T(8,128)(2,1)} %param.9, bf16[16,144,2560]{2,0,1:T(8,128)(2,1)} %all-gather.2.cloned.1.call-done), kind=kOutput, calls=%fused_computation.10.clone.clone.clone.1 | convolution fusion | flops 4535156736 | bytes 48562176 | tf_op jit(solution)/shard_map/erd,edf->erf/dot_general | solution.py:47
  217.1 16.3 %convert_bitcast_fusion = bf16[1,16,144,2560]{3,2,1,0:T(8,128)(2,1)} fusion(bf16[16,384,2560]{2,1,0:T(8,128)(2,1)} %param.11, bf16[16,144,384]{2,1,0:T(8,128)(2,1)S(1)} %multiply_convert_fusion.clone.4), kind=kOutput, calls=%fused_computation.3 | convolution fusion | flops 4535746560 | bytes 45023232 | tf_op jit(solution)/shard_map/erf,efd->erd/dot_general | solution.py:50
  233.4 17.0 %copy.28 = bf16[1,16,144,2560]{3,1,0,2:T(8,128)(2,1)S(1)} copy(bf16[1,16,144,2560]{3,2,1,0:T(8,128)(2,1)} %convert_bitcast_fusion) | data formatting | bytes 23592960 | tf_op jit(solution)/shard_map/broadcast_in_dim | solution.py:51
  250.4 133.5 %all_to_all.43 = bf16[1,16,144,2560]{3,1,0,2:T(8,128)(2,1)} all-to-all(bf16[1,16,144,2560]{3,1,0,2:T(8,128)(2,1)S(1)} %copy.28), channel_id=1, replica_groups=mesh['dp'=2,'ep'=4,'tp'=4] {'tp'}, dimensions={2} | all-to-all | bytes 23592960 | tf_op jit(solution)/shard_map/all_to_all | solution.py:51
  384.0 9.0 %reduce_sum.31 = bf16[16,36,2560]{2,0,1:T(8,128)(2,1)} reduce(bf16[16,4,36,2560]{3,0,2,1:T(8,128)(2,1)} %bitcast.37, bf16[]{:T(256)} %constant.48.clone.1), dimensions={1}, to_apply=%region_4.5 | reduce | flops 4423680 | bytes 14745602 | tf_op jit(solution)/shard_map/reduce_sum | solution.py:52
  393.0 4.7 all-to-all-start.2
  398.0 65.6 %all-to-all-done.2 = bf16[1,16,36,2560]{3,1,0,2:T(8,128)(2,1)S(1)} async-done(((bf16[1,16,36,2560]{3,1,0,2:T(8,128)(2,1)}), bf16[1,16,36,2560]{3,1,0,2:T(8,128)(2,1)S(1)}, u32[]{:S(2)}, u32[]{:S(2)}) %all-to-all-start.2) | async-done | bytes 2949152 | tf_op jit(solution)/shard_map/all_to_all | solution.py:53
  463.6 4.2 copy.29
  467.8 3.8 reshape.78
  471.6 3.1 gather_fusion.1
  474.7 2.4 reshape.89
  477.1 2.6 multiply_reduce_fusion
  (30 shorter events, 1.2 us)
Async XLA Ops:
  6.5 6.6 %copy-start = (bf16[48,2560]{1,0:T(8,128)(2,1)S(1)}, bf16[48,2560]{1,0:T(8,128)(2,1)}, u32[]{:S(2)}) copy-start(bf16[48,2560]{1,0:T(8,128)(2,1)} %param.6) | copy-start | bytes 737284
  6.5 168.6 %all-gather.2.cloned.1.call-start = ((), (), s32[]{:S(2)}) async-start(), calls=%async_computation.3 | async-start | bytes 14745600 | tf_op jit(solution)/shard_map/all_gather | solution.py:46
  393.0 4.7 copy-start.2
  393.0 70.5 %all-to-all-start.2 = ((bf16[1,16,36,2560]{3,1,0,2:T(8,128)(2,1)}), bf16[1,16,36,2560]{3,1,0,2:T(8,128)(2,1)S(1)}, u32[]{:S(2)}, u32[]{:S(2)}) async-start(bf16[1,16,36,2560]{3,1,0,2:T(8,128)(2,1)} %bitcast.6), calls=%async_computation.2 | async-start | bytes 5898240 | tf_op jit(solution)/shard_map/all_to_all | solution.py:53
  471.6 8.1 %copy-start.1 = (bf16[48,2560]{1,0:T(8,128)(2,1)S(1)}, bf16[48,2560]{1,0:T(8,128)(2,1)}, u32[]{:S(2)}) copy-start(bf16[48,2560]{1,0:T(8,128)(2,1)} %param.6) | copy-start | bytes 737284
Sparse Core Ops, SparseCore 0:
  97.6 77.4 all-gather.1
where the time goes:
time: 487 us
  blocking collectives  206 us (42%)
  waiting for transfers between devices  143 us (29%)
  matrix products  58.3 us (12%)
  local copies, waits for them, and re-layouts  44 us (9%)
  other arithmetic  16.6 us (3%)
  between operations  13.6 us (3%)
    all_to_all x1, blocking collectives, local_layer(): pieces = lax.all_to_all(part_sums[None], 'tp', 2, 0, tiled=True)  134 us
    all_gather x1, waiting for transfers between devices, local_layer(): group_rows = lax.all_gather(recv_rows, 'tp', axis=1, tiled=True)  77.6 us
    all_to_all x1, blocking collectives, local_layer(): recv_rows = lax.all_to_all(send_rows, 'ep', 0, 2, tiled=True)[0]  72.6 us
    all_to_all x1, waiting for transfers between devices, local_layer(): returned = lax.all_to_all(y_rows[None], 'ep', 2, 0, tiled=True)  65.6 us
    dot_general x1, matrix products, local_layer(): jnp.einsum('erd,edf->erf', group_rows, wu_loc, preferred_element_type=jnp...  21.1 us
    dot_general x1, matrix products, local_layer(): jnp.einsum('erd,edf->erf', group_rows, wg_loc, preferred_element_type=jnp...  20.8 us
    broadcast_in_dim x1, local copies, waits for them, and re-layouts, local_layer(): pieces = lax.all_to_all(part_sums[None], 'tp', 2, 0, tiled=True)  17 us
    dot_general x1, matrix products, local_layer(): jnp.einsum('erf,efd->erd', hidden, wd_loc, preferred_element_type=jnp.flo...  16.3 us
  transfers between devices with their start and end apart: 2, of which 2 were waited for; matrix products, arithmetic and copies ran while one was open for 0% of the time, Pallas kernels for 0%

commit v1 on v0

v1 whole, which is shorter than its diff:
```python
import functools

import jax
import jax.numpy as jnp
from jax import lax
from jax.experimental import pallas as pl
from jax.experimental.pallas import tpu as pltpu
from jax.sharding import PartitionSpec as P

CAP_FACTOR = 2
ROOM = 352
ROOM_PAD = 384
COLS = 256
W_SLOTS = 5
EXT = 256
MESH = pl.DeviceIdType.MESH
BF16 = jnp.bfloat16
F32 = jnp.float32


def slot_table(ids_loc, n_exp):
    tok_loc, n_top = ids_loc.shape
    flat_ids = ids_loc.reshape(tok_loc * n_top)
    one_hot = (flat_ids[:, None] == jnp.arange(n_exp, dtype=jnp.int32)[None, :]).astype(jnp.int32)
    preceding = jnp.cumsum(one_hot, axis=0) - one_hot
    return jnp.sum(preceding * one_hot, axis=1).reshape(tok_loc, n_top)


def padded_layer(x_loc, ids_loc, gate_loc, wg_loc, wu_loc, wd_loc, expert_ranks, tensor_ranks):
    tok_loc, d_model = x_loc.shape
    n_top = ids_loc.shape[1]
    local_exp = wg_loc.shape[0]
    n_exp = local_exp * expert_ranks
    capacity = CAP_FACTOR * n_top * tok_loc // n_exp
    slot_ids = slot_table(ids_loc, n_exp)
    kept_mask = slot_ids < capacity
    flat_pos = jnp.where(kept_mask, ids_loc * capacity + slot_ids, n_exp * capacity)
    tok_index = jnp.broadcast_to(jnp.arange(tok_loc, dtype=jnp.int32)[:, None], (tok_loc, n_top))
    src_rows = jnp.zeros((n_exp * capacity,), jnp.int32).at[flat_pos.reshape(-1)].set(tok_index.reshape(-1), mode="drop")
    send_rows = jnp.take(x_loc, src_rows, axis=0).reshape(expert_ranks, local_exp, capacity, d_model)
    recv_rows = lax.all_to_all(send_rows, "ep", 0, 2, tiled=True)[0]
    copies = jnp.broadcast_to(recv_rows[None], (tensor_ranks, *recv_rows.shape))
    group_rows = lax.all_to_all(copies, "tp", 0, 2, tiled=True)[0]
    gate_pre = jnp.einsum("erd,edf->erf", group_rows, wg_loc, preferred_element_type=F32)
    up_pre = jnp.einsum("erd,edf->erf", group_rows, wu_loc, preferred_element_type=F32)
    hidden = (jax.nn.silu(gate_pre) * up_pre).astype(BF16)
    part_sums = jnp.einsum("erf,efd->erd", hidden, wd_loc, preferred_element_type=F32).astype(BF16)
    pieces = lax.all_to_all(part_sums[None], "tp", 2, 0, tiled=True)
    y_rows = jnp.sum(pieces.astype(F32), axis=0).astype(BF16)
    returned = lax.all_to_all(y_rows[None], "ep", 2, 0, tiled=True)
    y_slots = returned.reshape(n_exp * capacity, d_model)
    picked = jnp.take(y_slots, jnp.where(kept_mask, flat_pos, 0), axis=0)
    weights = jnp.where(kept_mask, gate_loc, 0.0)
    return jnp.sum(picked.astype(F32) * weights[:, :, None], axis=1).astype(BF16)


def iota(shape, dim):
    return lax.broadcasted_iota(jnp.int32, shape, dim)


def dot(a, b):
    return jnp.dot(a, b, preferred_element_type=F32)


def mask(cond):
    return jnp.where(cond, 1.0, 0.0).astype(BF16)


def layer_kernel(
    x_hbm, ids_ref, gate_ref, wg_hbm, wu_hbm, wd_hbm,
    out_ref, flag_ref,
    xall, pmat, xg, wbuf, hbuf, wdbuf, part, pack, gmat, codes, tots, flag_in,
    own, send_s, recv_s, sum_0, send_y, recv_y, ybuf, send_z, recv_z,
    sem_x, sem_w, sem_wd, sem_xr, sem_xz, sem_xy, sem_xs,
    sem_ss, sem_rs, sem_sy, sem_ry, sem_sz, sem_rz, sem_f,
):
    d_model = x_hbm.shape[1]
    tok = ids_ref.shape[0]
    n_top = ids_ref.shape[1]
    n_loc, _, f_loc = wg_hbm.shape
    n_z = xall.shape[1]
    grp = n_z * tok
    cap = CAP_FACTOR * n_top * tok // (n_loc * n_z)
    cls = n_z * cap
    crow = xg.shape[2]
    n_chunk = d_model // COLS

    dp = lax.axis_index("dp")
    z = lax.axis_index("ep")
    k = lax.axis_index("tp")
    ks = k + 1 - 2 * lax.rem(k, 2)
    ky = lax.rem(k + 2, 4)
    ksy = lax.rem(ks + 2, 4)

    def w_copy(e, half):
        slot = lax.rem(e, W_SLOTS)
        src = wg_hbm if half == 0 else wu_hbm
        dst = wbuf.at[slot, :, pl.ds(half * f_loc, f_loc)]
        return pltpu.make_async_copy(src.at[e], dst, sem_w.at[slot, half])

    def wd_copy(i):
        slot = lax.rem(i, 2)
        src = wd_hbm.at[:, :, pl.ds(pl.multiple_of(i * COLS, COLS), COLS)]
        return pltpu.make_async_copy(src, wdbuf.at[slot], sem_wd.at[slot])

    x_copy = pltpu.make_async_copy(x_hbm, xall.at[k, z, :, pl.ds(0, d_model)], sem_x)
    x_copy.start()

    @pl.loop(0, W_SLOTS)
    def _(e):
        w_copy(e, 0).start()
        w_copy(e, 1).start()

    barrier = pltpu.get_barrier_semaphore()
    for j in range(1, n_z):
        pl.semaphore_signal(barrier, inc=1, device_id={"ep": lax.rem(z + j, n_z)}, device_id_type=MESH)
    for other in (ks, ky):
        pl.semaphore_signal(barrier, inc=1, device_id={"tp": other}, device_id_type=MESH)
    pl.semaphore_signal(barrier, inc=1, device_id={"dp": 1 - dp}, device_id_type=MESH)

    lane = iota((tok, 128), 1)
    chosen = jnp.zeros((tok, 128), F32)
    gates = jnp.zeros((tok, 128), F32)
    for j in range(n_top):
        hit = ids_ref[:, j : j + 1] == lane
        chosen = jnp.where(hit, 1.0, chosen)
        gates = jnp.where(hit, gate_ref[:, j : j + 1], gates)
    before = mask(iota((tok, tok), 0) > iota((tok, tok), 1))
    slots = dot(before, chosen.astype(BF16))
    kept = jnp.logical_and(chosen > 0.5, slots < cap)
    code = jnp.where(kept, slots + (cap * z).astype(F32), -1.0)
    g1 = gates.astype(BF16).astype(F32)
    g2 = (gates - g1).astype(BF16).astype(F32)
    g3 = gates - g1 - g2
    low = lane < 64
    first = jnp.where(low, code, pltpu.roll(g1, 64, 1))
    second = jnp.where(low, g2, pltpu.roll(g3, 64, 1))
    xall[k, z, :, pl.ds(d_model, 128)] = first.astype(BF16)
    xall[k, z, :, pl.ds(d_model + 128, 128)] = second.astype(BF16)
    ybuf[...] = jnp.zeros_like(ybuf)

    x_copy.wait()
    pl.semaphore_wait(barrier, n_z + 2)

    def x_send(kk, zz, to, sem):
        blk = xall.at[kk, zz]
        return pltpu.make_async_remote_copy(
            src_ref=blk, dst_ref=blk, send_sem=sem, recv_sem=sem_xr.at[kk, zz], device_id=to, device_id_type=MESH
        )

    def x_wait(kk, zz):
        x_send(kk, zz, {"tp": ks}, sem_xs.at[0, 0]).wait_recv()

    def to_right(zz):
        return x_send(k, zz, {"ep": z + 1}, sem_xz.at[0, zz])

    def to_left(zz):
        return x_send(k, zz, {"ep": z - 1}, sem_xz.at[1, zz])

    def to_y(zz):
        return x_send(k, zz, {"tp": ky}, sem_xy.at[zz])

    def to_sib(kk, zz, row):
        return x_send(kk, zz, {"tp": ks}, sem_xs.at[row, zz])

    @pl.when(z < n_z - 1)
    def _():
        to_right(z).start()

    @pl.when(z > 0)
    def _():
        to_left(z).start()

    to_y(z).start()
    to_sib(k, z, 0).start()

    def y_arrived(zz):
        x_wait(ky, zz)
        to_sib(ky, zz, 1).start()

    for j in range(1, n_z):

        @pl.when(z - j >= 0)
        def _():
            x_wait(k, z - j)

            @pl.when(z < n_z - 1)
            def _():
                to_right(z - j).start()

            to_y(z - j).start()
            to_sib(k, z - j, 0).start()

        @pl.when(z + j < n_z)
        def _():
            x_wait(k, z + j)

            @pl.when(z > 0)
            def _():
                to_left(z + j).start()

            to_y(z + j).start()
            to_sib(k, z + j, 0).start()

        if j == 1:
            y_arrived(z)
        else:

            @pl.when(z - j + 1 >= 0)
            def _():
                y_arrived(z - j + 1)

            @pl.when(z + j - 1 < n_z)
            def _():
                y_arrived(z + j - 1)

    def gather(kk):
        ext = xall[kk, :, :, pl.ds(d_model, 128)].reshape(grp, 128)
        pick_e = mask(iota((n_loc, 128), 1) == iota((n_loc, 128), 0) + z * n_loc)
        code_t = lax.dot_general(pick_e, ext, (((1,), (1,)), ((), ())), preferred_element_type=F32)
        row = iota((n_loc, crow, grp), 1).astype(F32)
        pmat[...] = jnp.where(code_t[:, None, :] == row, 1.0, 0.0).astype(BF16).reshape(n_loc * crow, grp)

        @pl.loop(0, d_model // 512)
        def _(n):
            at = pl.ds(pl.multiple_of(n * 512, 512), 512)
            got = dot(pmat[...], xall[kk, :, :, at].reshape(grp, 512))
            xg[:, kk, :, at] = got.astype(BF16).reshape(n_loc, crow, 512)

        kept_t = mask(code_t >= 0.0)
        lane_m = iota((grp, 128), 1)
        from_z = iota((grp, 128), 0) // tok
        lane_z = lane_m // cap
        valid = lane_m < cls
        count = dot(kept_t, mask(jnp.logical_and(lane_z == from_z, valid)))
        prior_z = dot(kept_t, mask(jnp.logical_and(from_z < lane_z, valid)))
        total = dot(kept_t, jnp.ones((grp, 128), BF16))
        below = mask(iota((n_loc, n_loc), 0) > iota((n_loc, n_loc), 1))
        base = dot(below, total.astype(BF16)) + prior_z
        m_lane = iota((n_loc, 128), 1)
        slot = (m_lane - cap * (m_lane // cap)).astype(F32)
        pos = jnp.where(jnp.logical_and(slot < count, m_lane < cls), base + slot, -1.0)
        high = jnp.floor(pos * (1.0 / 32.0))
        lowp = pos - 32.0 * high
        width = n_loc * crow
        lane_w = iota((128, width), 1)
        spread = mask(lane_w - crow * (lane_w // crow) == iota((128, width), 0))
        wide = 32.0 * dot(high.astype(BF16), spread) + dot(lowp.astype(BF16), spread)
        here = iota((n_loc, width), 1) // crow == iota((n_loc, width), 0)
        pos_row = jnp.sum(jnp.where(here, wide, 0.0), axis=0, keepdims=True)
        pack[kk] = jnp.where(pos_row == iota((ROOM, width), 0).astype(F32), 1.0, 0.0).astype(BF16)

        kept_n = mask(jnp.logical_and(ext.astype(F32) >= 0.0, iota((grp, 128), 1) < 64))
        per_e = dot(jnp.ones((8, grp), BF16), kept_n)
        same = mask(iota((128, 128), 0) // n_loc == iota((128, 128), 1) // n_loc)
        return dot(per_e.astype(BF16), same)

    tot = gather(k)
    for zz in range(n_z):
        x_wait(ks, zz)
    tot = jnp.maximum(tot, gather(ks))

    @pl.when(z == 0)
    def _():
        y_arrived(n_z - 1)

    @pl.when(z == n_z - 1)
    def _():
        y_arrived(0)

    tot = jnp.maximum(tot, gather(ky))
    for zz in range(n_z):
        x_wait(ksy, zz)
    tots[...] = jnp.maximum(tot, gather(ksy))
    f_copy = pltpu.make_async_remote_copy(
        src_ref=tots, dst_ref=flag_in, send_sem=sem_f.at[0], recv_sem=sem_f.at[1],
        device_id={"dp": 1 - dp}, device_id_type=MESH,
    )

    wd_copy(0).start()
    wd_copy(1).start()

    pick_n = mask(iota((128, 128), 0) == iota((128, 128), 1) + z * n_loc)
    pick_h = mask(iota((128, 128), 0) == iota((128, 128), 1) + z * n_loc + 64)
    in_e = iota((tok, 128), 1) < n_loc
    kept_all = []
    for zz in range(n_z):
        code_n = dot(xall[k, zz, :, pl.ds(d_model, 128)], pick_n)
        kept_all.append(jnp.logical_and(code_n >= 0.0, in_e))
        codes[zz] = code_n - float(cap * zz)
    counts = [dot(jnp.ones((tok, tok), BF16), mask(kz)) for kz in kept_all]
    all_cnt = counts[0]
    for c in counts[1:]:
        all_cnt = all_cnt + c
    base_e = dot(all_cnt.astype(BF16), mask(iota((128, 128), 0) < iota((128, 128), 1)))
    prior = jnp.zeros((tok, 128), F32)
    p_lane = iota((tok, ROOM_PAD), 1).astype(F32)
    for zz in range(n_z):
        pos = jnp.where(kept_all[zz], base_e + prior + codes[zz], -1.0)
        prior = prior + counts[zz]
        e0 = xall[k, zz, :, pl.ds(d_model, 128)]
        e1 = xall[k, zz, :, pl.ds(d_model + 128, 128)]
        terms = (dot(e0, pick_h), dot(e1, pick_n), dot(e1, pick_h))
        acc = [jnp.zeros((tok, ROOM_PAD), F32) for _ in terms]
        for e in range(n_loc):
            hit = pos[:, e : e + 1] == p_lane
            acc = [jnp.where(hit, t[:, e : e + 1], a) for t, a in zip(terms, acc)]
        for i, a in enumerate(acc):
            gmat[zz, i] = a.astype(BF16)

    f_copy.start()

    @pl.loop(0, n_loc)
    def _(e):
        w_copy(e, 0).wait()
        w_copy(e, 1).wait()
        both = dot(xg[e].reshape(4 * crow, d_model), wbuf[lax.rem(e, W_SLOTS)])
        a, b = both[:, :f_loc], both[:, f_loc:]
        hbuf[e] = (a / (1.0 + jnp.exp(-a)) * b).astype(BF16)

        @pl.when(e + W_SLOTS < n_loc)
        def _():
            w_copy(e + W_SLOTS, 0).start()
            w_copy(e + W_SLOTS, 1).start()

    def s_copy(i):
        return pltpu.make_async_remote_copy(
            src_ref=send_s.at[lax.rem(i, 2)], dst_ref=recv_s.at[i], send_sem=sem_ss.at[lax.rem(i, 2)],
            recv_sem=sem_rs.at[i], device_id={"tp": ks}, device_id_type=MESH,
        )

    def y_copy(i):
        return pltpu.make_async_remote_copy(
            src_ref=send_y.at[lax.rem(i, 2)], dst_ref=recv_y.at[i], send_sem=sem_sy.at[lax.rem(i, 2)],
            recv_sem=sem_ry.at[i], device_id={"tp": ky}, device_id_type=MESH,
        )

    def z_copy(i, j):
        to = lax.rem(z + j, n_z)
        return pltpu.make_async_remote_copy(
            src_ref=send_z.at[lax.rem(i, 2), to], dst_ref=recv_z.at[i, j - 1], send_sem=sem_sz.at[lax.rem(i, 2), j - 1],
            recv_sem=sem_rz.at[i, j - 1], device_id={"ep": to}, device_id_type=MESH,
        )

    def down(i):
        par = lax.rem(i, 2)
        wd_copy(i).wait()

        @pl.loop(0, n_loc)
        def _(e):
            got = dot(hbuf[e], wdbuf[par, e])
            part[:, e] = got.astype(BF16).reshape(4, crow, COLS)

        @pl.when(i + 2 < n_chunk)
        def _():
            wd_copy(i + 2).start()

        @pl.when(i >= 2)
        def _():
            s_copy(i - 2).wait_send()

        def packed(kk):
            return dot(pack[kk], part[kk].reshape(n_loc * crow, COLS)).astype(BF16)

        send_s[par, 0] = packed(ks)
        send_s[par, 1] = packed(ksy)
        s_copy(i).start()
        own[par, 0] = packed(k)
        own[par, 1] = packed(ky)

    def across_y(i):
        par = lax.rem(i, 2)
        s_copy(i).wait_recv()

        @pl.when(i >= 2)
        def _():
            y_copy(i - 2).wait_send()

        send_y[par] = (own[par, 1].astype(F32) + recv_s[i, 1].astype(F32)).astype(BF16)
        y_copy(i).start()
        sum_0[par] = own[par, 0].astype(F32) + recv_s[i, 0].astype(F32)

    def across_z(i):
        par = lax.rem(i, 2)
        y_copy(i).wait_recv()
        ybuf[pl.ds(0, ROOM), :] = (sum_0[par] + recv_y[i].astype(F32)).astype(BF16)

        @pl.when(i >= 2)
        def _():
            for j in range(1, n_z):
                z_copy(i - 2, j).wait_send()

        got = dot(gmat[...].reshape(n_z * 3 * tok, ROOM_PAD), ybuf[...]).reshape(n_z, 3, tok, COLS)
        send_z[par] = (got[:, 2] + got[:, 1]) + got[:, 0]
        for j in range(1, n_z):
            z_copy(i, j).start()

    def finish(i):
        for j in range(1, n_z):
            z_copy(i, j).wait_recv()
        out = send_z[lax.rem(i, 2), z]
        for j in range(1, n_z):
            out = out + recv_z[i, j - 1]
        out_ref[:, pl.ds(pl.multiple_of(i * COLS, COLS), COLS)] = out.astype(BF16)

    @pl.loop(0, n_chunk + 3)
    def _(it):
        @pl.when(it < n_chunk)
        def _():
            down(it)

        @pl.when(jnp.logical_and(it >= 1, it < n_chunk + 1))
        def _():
            across_y(it - 1)

        @pl.when(jnp.logical_and(it >= 2, it < n_chunk + 2))
        def _():
            across_z(it - 2)

        @pl.when(it >= 3)
        def _():
            finish(it - 3)

    f_copy.wait()
    flag_ref[...] = jnp.maximum(tots[...], flag_in[...])
    for i in (n_chunk - 2, n_chunk - 1):
        s_copy(i).wait_send()
        y_copy(i).wait_send()
        for j in range(1, n_z):
            z_copy(i, j).wait_send()

    @pl.loop(0, n_z)
    def _(zz):
        @pl.when(jnp.logical_and(z < n_z - 1, zz <= z))
        def _():
            to_right(zz).wait_send()

        @pl.when(jnp.logical_and(z > 0, zz >= z))
        def _():
            to_left(zz).wait_send()

        to_y(zz).wait_send()
        to_sib(k, zz, 0).wait_send()
        to_sib(ky, zz, 1).wait_send()


def packed_layer(n_z, x_loc, ids_loc, gate_loc, wg_loc, wu_loc, wd_loc):
    tok, d_model = x_loc.shape
    n_loc, _, f_loc = wg_loc.shape
    n_top = ids_loc.shape[1]
    cap = CAP_FACTOR * n_top * tok // (n_loc * n_z)
    crow = -(-n_z * cap // 16) * 16
    n_chunk = d_model // COLS
    wide = d_model + EXT
    dma = pltpu.SemaphoreType.DMA
    return pl.pallas_call(
        layer_kernel,
        out_shape=(jax.ShapeDtypeStruct((tok, d_model), BF16), jax.ShapeDtypeStruct((8, 128), F32)),
        in_specs=[
            pl.BlockSpec(memory_space=pl.ANY),
            pl.BlockSpec(memory_space=pltpu.VMEM),
            pl.BlockSpec(memory_space=pltpu.VMEM),
            pl.BlockSpec(memory_space=pl.ANY),
            pl.BlockSpec(memory_space=pl.ANY),
            pl.BlockSpec(memory_space=pl.ANY),
        ],
        out_specs=(pl.BlockSpec(memory_space=pltpu.VMEM), pl.BlockSpec(memory_space=pltpu.VMEM)),
        scratch_shapes=[
            pltpu.VMEM((4, n_z, tok, wide), BF16),
            pltpu.VMEM((n_loc * crow, n_z * tok), BF16),
            pltpu.VMEM((n_loc, 4, crow, d_model), BF16),
            pltpu.VMEM((W_SLOTS, d_model, 2 * f_loc), BF16),
            pltpu.VMEM((n_loc, 4 * crow, f_loc), BF16),
            pltpu.VMEM((2, n_loc, f_loc, COLS), BF16),
            pltpu.VMEM((4, n_loc, crow, COLS), BF16),
            pltpu.VMEM((4, ROOM, n_loc * crow), BF16),
            pltpu.VMEM((n_z, 3, tok, ROOM_PAD), BF16),
            pltpu.VMEM((n_z, tok, 128), F32),
            pltpu.VMEM((8, 128), F32),
            pltpu.VMEM((8, 128), F32),
            pltpu.VMEM((2, 2, ROOM, COLS), BF16),
            pltpu.VMEM((2, 2, ROOM, COLS), BF16),
            pltpu.VMEM((n_chunk, 2, ROOM, COLS), BF16),
            pltpu.VMEM((2, ROOM, COLS), F32),
            pltpu.VMEM((2, ROOM, COLS), BF16),
            pltpu.VMEM((n_chunk, ROOM, COLS), BF16),
            pltpu.VMEM((ROOM_PAD, COLS), BF16),
            pltpu.VMEM((2, n_z, tok, COLS), F32),
            pltpu.VMEM((n_chunk, n_z - 1, tok, COLS), F32),
            dma,
            dma((W_SLOTS, 2)),
            dma((2,)),
            dma((4, n_z)),
            dma((2, n_z)),
            dma((n_z,)),
            dma((2, n_z)),
            dma((2,)),
            dma((n_chunk,)),
            dma((2,)),
            dma((n_chunk,)),
            dma((2, n_z - 1)),
            dma((n_chunk, n_z - 1)),
            dma((2,)),
        ],
        compiler_params=pltpu.CompilerParams(collective_id=0, has_side_effects=True, vmem_limit_bytes=67043328),
        name="moe_layer",
    )(x_loc, ids_loc, gate_loc, wg_loc, wu_loc, wd_loc)


def solution(mesh):
    expert_ranks, tensor_ranks = mesh.shape["ep"], mesh.shape["tp"]
    row_spec = P(("dp", "ep", "tp"), None)

    def local_layer(*args):
        out, totals = packed_layer(expert_ranks, *args)
        fits = jnp.max(totals) <= ROOM
        return lax.cond(
            fits,
            lambda out, *args: out,
            lambda out, *args: padded_layer(*args, expert_ranks, tensor_ranks),
            out,
            *args,
        )

    return jax.shard_map(local_layer, mesh=mesh, in_specs=(row_spec, row_spec, row_spec, P("ep", None, "tp"), P("ep", None, "tp"), P("ep", "tp", None)), out_specs=row_spec, check_vma=False)
```

time: 487 us -> 133 us (0.27)
  blocking collectives: 206 us -> 0 us
  waiting for transfers between devices: 143 us -> 0 us
  Pallas kernels: 0 us -> 127 us
  matrix products: 58.3 us -> 0 us
  local copies, waits for them, and re-layouts: 44 us -> 4.4 us
  other arithmetic: 16.6 us -> 1.28 us
  between operations: 13.6 us -> 0.67 us
    all_to_all x2 -> x0, blocking collectives: 206 us -> none  [the longest x1 134 us: local_layer(): pieces = lax.all_to_all(part_sums[None], 'tp', 2, 0, tiled=True)]
    pallas_call x0 -> x1, Pallas kernels: none -> 127 us  [packed_layer(): pl.pallas_call(layer_kernel, out_shape=(jax.ShapeDtypeStruct((tok, d_mode...]
    all_gather x1 -> x0, waiting for transfers between devices: 77.6 us -> none  [local_layer(): group_rows = lax.all_gather(recv_rows, 'tp', axis=1, tiled=True)]
    all_to_all x1 -> x0, waiting for transfers between devices: 65.6 us -> none  [local_layer(): returned = lax.all_to_all(y_rows[None], 'ep', 2, 0, tiled=True)]
    dot_general x3 -> x0, matrix products: 58.3 us -> none  [the longest x1 21.1 us: local_layer(): jnp.einsum('erd,edf->erf', group_rows, wu_loc, preferred_element_type=jnp...]
    broadcast_in_dim x4 -> x0, local copies, waits for them, and re-layouts: 17.3 us -> none  [the longest x1 17 us: local_layer(): pieces = lax.all_to_all(part_sums[None], 'tp', 2, 0, tiled=True)]
    gather x4 -> x0, local copies, waits for them, and re-layouts: 12.4 us -> none  [the longest x2 6.85 us: local_layer(): jnp.take(x_loc, src_rows, axis=0)]
    reduce_sum x3 -> x0, other arithmetic: 11.7 us -> none  [the longest x1 9.04 us: local_layer(): y_rows = jnp.sum(pieces.astype(jnp.float32), axis=0).astype(jnp.bfloat16)]
  transfers between devices with their start and end apart: 2 -> 0, of which waited for: 2 -> 0; matrix products, arithmetic and copies ran while one was open for 0% -> 0% of each run, Pallas kernels for 0% -> 0%
where the time goes in v1:
time: 133 us
  Pallas kernels  127 us (95%)
  local copies, waits for them, and re-layouts  4.4 us (3%)
    pallas_call x1, Pallas kernels, packed_layer(): pl.pallas_call(layer_kernel, out_shape=(jax.ShapeDtypeStruct((tok, d_mode...  127 us
    unnamed x3, local copies, waits for them, and re-layouts  4.4 us

profile of v1, /device:TPU:0, one launch (start us, length us, event | category | flops | bytes accessed | tf_op | source)
XLA Modules:
  0.0 133.1 jit_solution(8340423872375182432)
XLA Ops:
  0.0 1.4 %copy.30.ids_ref = s32[48,6]{1,0:T(8,128)} copy(s32[48,6]{0,1:T(8,128)} %param.9) | data formatting | bytes 2304 | tf_op args[1]
  1.4 1.4 %copy.31.gate_ref = f32[48,6]{1,0:T(8,128)} copy(f32[48,6]{0,1:T(8,128)} %param.10) | data formatting | bytes 2304 | tf_op args[2]
  2.7 126.6 %moe_layer.1 = (bf16[48,2560]{1,0:T(8,128)(2,1)}, f32[8,128]{1,0:T(8,128)}) custom-call(bf16[48,2560]{1,0:T(8,128)(2,1)} %x_hbm.1, s32[48,6]{1,0:T(8,128)} %copy.30.ids_ref, f32[48,6]{1,0:T(8,128)} %copy.31.gate_ref, bf16[16,2560,384]{2,1,0:T(8,128)(2,1)} %wg_hbm.1, bf16[16,2560,384]{2,1,0:T(8,128)(2,1)} %wu_hbm.1, bf16[16,384,2560]{2,1,0:T(8,128)(2,1)} %wd_hbm.1), custom_call_target="tpu_custom_call" | custom-call | tf_op jit(solution)/shard_map/moe_layer/pallas_call | solution.py:456
  129.3 1.3 reduce_max.9
  131.2 0.2 conditional.1
  131.5 1.7 %copy.52 = bf16[48,2560]{1,0:T(8,128)(2,1)} copy(bf16[48,2560]{1,0:T(8,128)(2,1)} %get-tuple-element.31) | data formatting | bytes 491520
